TPU v7x, 32 devices: a whole 2x2x4 slice. The times are simulated.
32 devices in a mesh: rep: 4 (over z), rows: 8 (over y, x, core).
Axes of the slice: x: 2, y: 2, z: 4, core: 2. Of those that a mesh axis runs over, the one named last changes fastest.
Arguments:
- adjacency: bfloat16 [24576, 24576], P('rows', 'rep')
- block_mask: int32 [8, 8], replicated
- features: bfloat16 [24576, 100], P('rows')
- w_one: bfloat16 [100, 256], replicated
- w_two: bfloat16 [256, 47], replicated
Outputs:
- output: float32 [24576, 47], P('rows')
All inputs are finite; a program needn't handle non-finite values.
Results may differ from a plain program's by a relative error of at most 0.001.
Values are sent between devices in bfloat16 or wider.
A program may use at most 1 GiB of HBM per device.

v0:
```python
import jax
import jax.numpy as jnp
from jax import lax
from jax.sharding import PartitionSpec as P


def solution(mesh):
    rep_size = mesh.shape['rep']
    rows_size = mesh.shape['rows']
    stage_count = rows_size // rep_size
    perm_pairs = [(src_rep * rows_size + src_row, (src_row // stage_count) * rows_size + (src_row % stage_count) * rep_size + src_rep) for src_rep in range(rep_size) for src_row in range(rows_size)]

    def range_rows(feat_blk):
        rep_idx = lax.axis_index('rep')
        piece_rows = feat_blk.shape[0] // rep_size
        send_piece = lax.dynamic_slice_in_dim(feat_blk, rep_idx * piece_rows, piece_rows, 0)
        recv_piece = lax.ppermute(send_piece, ('rep', 'rows'), perm_pairs)
        return lax.all_gather(recv_piece, 'rows', axis=0, tiled=True)

    def aggregate(adj_local, block_mask, feat_blk):
        rows_idx = lax.axis_index('rows')
        rep_idx = lax.axis_index('rep')
        gathered = range_rows(feat_blk)
        blk_rows = feat_blk.shape[0]
        feat_width = feat_blk.shape[1]
        mask_part = lax.dynamic_slice(block_mask, (rows_idx, rep_idx * stage_count), (1, stage_count))
        masked = (gathered.reshape(stage_count, blk_rows, feat_width) * mask_part.astype(gathered.dtype).reshape(stage_count, 1, 1)).reshape(stage_count * blk_rows, feat_width)
        part_sum = jnp.dot(adj_local, masked, preferred_element_type=jnp.float32)
        return lax.psum(part_sum, 'rep').astype(jnp.bfloat16)

    def local_fn(adj_local, block_mask, feat_blk, w_one, w_two):
        y_one = aggregate(adj_local, block_mask, feat_blk)
        z_one = jnp.maximum(jnp.dot(y_one, w_one, preferred_element_type=jnp.float32), 0.0).astype(jnp.bfloat16)
        y_two = aggregate(adj_local, block_mask, z_one)
        return jnp.dot(y_two, w_two, preferred_element_type=jnp.float32)

    return jax.shard_map(local_fn, mesh=mesh, in_specs=(P('rows', 'rep'), P(), P('rows', None), P(), P()), out_specs=P('rows', None), check_vma=False)
```

profile of v0, /device:TPU:0, one launch (start us, length us, event | category | flops | bytes accessed | tf_op | source)
XLA Modules:
  0.0 319.2 jit_solution(3774970751709378019)
XLA Ops:
  6.5 0.0 copy-start
  6.5 0.0 all-gather.3.cloned.1.call-start
  6.5 1.1 copy-done
  7.6 0.7 collective-permute-start
  8.3 0.0 collective-permute-done
  8.3 0.0 copy-start.2
  8.3 0.7 copy-done.2
  9.0 0.0 all-gather.3.cloned.1.call-update
  9.0 0.0 all-gather.5.cloned.1.call-start
  9.1 0.8 convert_bitcast_fusion
  9.8 0.1 broadcast_bitcast_fusion
  9.9 39.8 %all-gather.3.cloned.1.call-done = bf16[6144,100]{0,1:T(8,128)(2,1)} async-done(((bf16[768,100]{0,1:T(8,128)(2,1)}), bf16[6144,100]{0,1:T(8,128)(2,1)}) %all-gather.3.cloned.1.call-update) | async-done | bytes 1228816 | tf_op jit(solution)/shard_map/all_gather | solution.py:18
  49.7 0.0 copy-start.3
  49.7 17.5 %convolution_bitcast_fusion.1 = f32[3072,100]{0,1:T(8,128)S(1)} fusion(bf16[3072,6144]{1,0:T(8,128)(2,1)} %param.5, bf16[6144,100]{0,1:T(8,128)(2,1)} %all-gather.3.cloned.1.call-done, bf16[6144]{0:T(1024)(128)(2,1)S(1)} %bitcast.15), kind=kOutput, calls=%fused_computation.1 | convolution fusion | flops 3775488000 | bytes 40218624 | tf_op jit(solution)/shard_map/dot_general | solution.py:28
  67.3 51.3 %all-reduce.2 = bf16[3072,100]{0,1:T(8,128)(2,1)S(1)} all-reduce(f32[3072,100]{0,1:T(8,128)S(1)} %convolution_bitcast_fusion.1), channel_id=1, replica_groups=mesh['rep'=4,'rows'=8] {'rep'}, use_global_device_ids=true, to_apply=%region_0.0 | all-reduce | flops 307200 | bytes 1843200 | tf_op jit(solution)/shard_map/psum | solution.py:29
  118.6 0.0 copy-done.3
  118.6 0.6 fusion.10
  119.2 0.1 fusion.5
  119.3 0.7 collective-permute-start.1
  120.0 0.0 collective-permute-done.1
  120.0 0.0 copy-start.1
  120.0 0.7 copy-done.1
  120.8 0.0 all-gather.5.cloned.1.call-update
  120.8 57.3 %all-gather.5.cloned.1.call-done = bf16[6144,256]{1,0:T(8,128)(2,1)} async-done(((bf16[768,256]{1,0:T(8,128)(2,1)}), bf16[6144,256]{1,0:T(8,128)(2,1)}) %all-gather.5.cloned.1.call-update) | async-done | bytes 3145744 | tf_op jit(solution)/shard_map/all_gather | solution.py:18
  178.1 20.2 %convolution_bitcast_fusion = f32[3072,256]{0,1:T(8,128)} fusion(bf16[3072,6144]{1,0:T(8,128)(2,1)} %param.5, bf16[6144,256]{1,0:T(8,128)(2,1)} %all-gather.5.cloned.1.call-done, bf16[6144]{0:T(1024)(128)(2,1)S(1)} %bitcast.16), kind=kOutput, calls=%fused_computation | convolution fusion | flops 9665249280 | bytes 44052480 | tf_op jit(solution)/shard_map/dot_general | solution.py:28
  198.3 0.0 copy-start.4
  198.3 112.8 %all-reduce.3 = bf16[3072,256]{0,1:T(8,128)(2,1)S(1)} all-reduce(f32[3072,256]{0,1:T(8,128)} %convolution_bitcast_fusion), channel_id=1, replica_groups=mesh['rep'=4,'rows'=8] {'rep'}, use_global_device_ids=true, to_apply=%region_1.0 | all-reduce | flops 786432 | bytes 4718592 | tf_op jit(solution)/shard_map/psum | solution.py:29
  311.1 0.0 copy-done.4
  311.1 1.2 fusion.9
  (2 shorter events, 0.0 us)
Async XLA Ops:
  6.5 1.1 copy-start
  6.5 43.2 %all-gather.3.cloned.1.call-start = ((), (), s32[]{:S(2)}) async-start(), calls=%async_computation | async-start | bytes 1437696 | tf_op jit(solution)/shard_map/all_gather | solution.py:18
  7.6 0.7 collective-permute-start
  8.3 0.7 copy-start.2
  9.0 169.1 %all-gather.5.cloned.1.call-start = ((), (), s32[]{:S(2)}) async-start(), calls=%async_computation.1 | async-start | bytes 3538944 | tf_op jit(solution)/shard_map/all_gather | solution.py:18
  49.7 68.9 %copy-start.3 = (bf16[100,256]{1,0:T(8,128)(2,1)S(1)}, bf16[100,256]{1,0:T(8,128)(2,1)}, u32[]{:S(2)}) copy-start(bf16[100,256]{1,0:T(8,128)(2,1)} %param.8) | copy-start | bytes 153604
  119.3 0.7 collective-permute-start.1
  120.0 0.7 copy-start.1
  198.3 112.8 %copy-start.4 = (bf16[256,47]{0,1:T(8,128)(2,1)S(1)}, bf16[256,47]{0,1:T(8,128)(2,1)}, u32[]{:S(2)}) copy-start(bf16[256,47]{0,1:T(8,128)(2,1)} %param.9) | copy-start | bytes 72196
Sparse Core Ops, SparseCore 0:
  9.2 40.4 all-gather.2
  120.9 57.1 all-gather.4
where the time goes:
time: 320 us; the launch traced here: 319 us
  blocking collectives  164 us (51%)
  waiting for transfers between devices  97.2 us (30%)
  matrix products  39.5 us (12%)
  between operations  13.5 us (4%)
    psum x2, blocking collectives, aggregate(): return lax.psum(part_sum, 'rep').astype(jnp.bfloat16)  164 us
    all_gather x2, waiting for transfers between devices, range_rows(): return lax.all_gather(recv_piece, 'rows', axis=0, tiled=True)  97.1 us
    dot_general x2, matrix products, aggregate(): part_sum = jnp.dot(adj_local, masked, preferred_element_type=jnp.float32)  37.7 us
  transfers between devices with their start and end apart: 4, of which 2 were waited for; matrix products, arithmetic and copies ran while one was open for 0% of the time, Pallas kernels for 0%

commit v1 on v0

v1 whole, which is shorter than its diff:
```python
import functools

import jax
import jax.numpy as jnp
from jax import lax
from jax.experimental import pallas as pl
from jax.experimental.pallas import tpu as pltpu
from jax.sharding import PartitionSpec as P

MESH = pl.DeviceIdType.MESH
BF16 = jnp.bfloat16
F32 = jnp.float32
SUB = 64
OUT_COLS = 128
S_LAG, OS_LAG, OF_LAG = 4, 12, 16


def dot(a, b, dims):
    return lax.dot_general(a, b, (dims, ((), ())), preferred_element_type=F32)


def kernel(mask_ref, adj_hbm, featt_ref, w1_ref, w2t_ref, outt_ref,
           adj, ht, w1p, w2p, pbuf, dbuf, xbuf, ybuf, yt, zt, y2, r_first, r_second, ot,
           adj_sem, ds_sem, dr_sem, xs_sem, xr_sem, ys_sem, yr_sem,
           gs_sem, gr_sem, fs_sem, fr_sem, ss_sem, sr_sem, us_sem, ur_sem, vs_sem, vr_sem):
    f0 = featt_ref.shape[0]
    f2 = w2t_ref.shape[0]
    f0p = ht.shape[0]
    f0s = pbuf.shape[2]
    blk, width = adj.shape
    chunk = width // 8
    half = chunk // 2
    rows_half = blk // 2
    mm_rows = blk // 8
    n_sub = rows_half // SUB
    sub_mm = mm_rows // SUB
    n_out = rows_half // OUT_COLS
    out_sub = OUT_COLS // SUB

    z = lax.axis_index('rep')
    r = lax.axis_index('rows')
    c = lax.rem(r, 2)
    x = lax.rem(r // 2, 2)
    y = r // 4
    core_p = r + 1 - 2 * c
    x_p = r + 2 - 4 * x
    y_p = r + 4 - 8 * y

    def rows_dev(i):
        return {'rows': i, 'rep': z}

    def rep_dev(i):
        return {'rows': r, 'rep': i}

    def order(k):
        ky, kx = lax.rem(k, 2), k // 2
        cy = y * ky + (1 - y) * (1 - ky)
        cx = x * kx + (1 - x) * (1 - kx)
        return 4 * cy + 2 * cx

    def chunk_of(s):
        side = s // 4
        return order(lax.rem(s, 4)) + (1 - c) * (1 - side) + c * side

    def chunk_cols(q):
        return pl.ds(pl.multiple_of(q * chunk, 128), chunk)

    def adj_copy(s):
        cols = chunk_cols(chunk_of(s))
        return pltpu.make_async_copy(adj_hbm.at[:, cols], adj.at[:, cols], adj_sem.at[s])

    for s in range(3):
        adj_copy(s).start()

    barrier = pltpu.get_barrier_semaphore()
    for dev in (core_p, x_p, y_p):
        pl.semaphore_signal(barrier, inc=1, device_id=rows_dev(dev), device_id_type=MESH)
    for dev in (lax.rem(z + 1, 4), lax.rem(z + 3, 4)):
        pl.semaphore_signal(barrier, inc=1, device_id=rep_dev(dev), device_id_type=MESH)

    ht[...] = jnp.zeros_like(ht)
    ht[0:f0, :] = featt_ref[...]
    w1p[...] = jnp.zeros_like(w1p)
    w1p[0:f0, :] = w1_ref[...]
    w2p[...] = jnp.zeros_like(w2p)
    w2p[0:f2, :] = w2t_ref[...]

    pl.semaphore_wait(barrier, 5)

    def remote(src, dst, send, recv, dev):
        return pltpu.make_async_remote_copy(
            src_ref=src, dst_ref=dst, send_sem=send, recv_sem=recv, device_id=dev, device_id_type=MESH)

    def core_copy(k):
        return remote(pbuf.at[k], dbuf.at[k], ds_sem.at[k], dr_sem.at[k], rows_dev(core_p))

    def x_copy(k, src):
        return remote(src, xbuf.at[k], xs_sem.at[k], xr_sem.at[k], rows_dev(x_p))

    def y_copy(k, src):
        return remote(src, ybuf.at[k], ys_sem.at[k], yr_sem.at[k], rows_dev(y_p))

    def layer_one(s, carry):
        q = chunk_of(s)
        adj_copy(s).wait()

        @pl.when(s < 5)
        def _():
            adj_copy(s + 3).start()

        keep = mask_ref[r, 2 * z + q // 4].astype(F32)
        part = dot(ht[...], adj[:, chunk_cols(q)], ((1,), (0,)))[0:f0s, :] * keep
        pbuf[s, 0] = part[:, 0:half]
        pbuf[s, 1] = part[:, half:chunk]

        @pl.when(s < 4)
        def _():
            core_copy(s).start()

        @pl.when(s >= 4)
        def _():
            core_copy(s - 4).wait_recv()
            pbuf[s] = pbuf[s] + dbuf[s - 4]

        @pl.when(s == 4)
        def _():
            x_copy(0, pbuf.at[4, 0]).start()
            y_copy(0, pbuf.at[4, 1]).start()

        @pl.when(s == 5)
        def _():
            x_copy(1, pbuf.at[5, 0]).start()

        @pl.when(s == 6)
        def _():
            y_copy(1, pbuf.at[6, 1]).start()

        return carry

    lax.fori_loop(0, 8, layer_one, 0)

    y_copy(0, pbuf.at[4, 1]).wait_recv()
    pbuf[5, 1] = pbuf[5, 1] + ybuf[0]
    x_copy(2, pbuf.at[5, 1]).start()
    x_copy(0, pbuf.at[4, 0]).wait_recv()
    pbuf[6, 0] = pbuf[6, 0] + xbuf[0]
    y_copy(2, pbuf.at[6, 0]).start()
    x_copy(1, pbuf.at[5, 0]).wait_recv()
    y_copy(1, pbuf.at[6, 1]).wait_recv()
    pbuf[7, 0] = pbuf[7, 0] + xbuf[1]
    pbuf[7, 1] = pbuf[7, 1] + ybuf[1]
    pad = jnp.zeros((f0p - f0s, half), F32)

    def own_cols(q, h):
        return pl.ds(pl.multiple_of(q * chunk + h * half, 128), half)

    x_copy(2, pbuf.at[5, 1]).wait_recv()
    yt[:, own_cols(r, 1)] = jnp.concatenate([pbuf[7, 1] + xbuf[2], pad], axis=0).astype(BF16)
    y_copy(2, pbuf.at[6, 0]).wait_recv()
    yt[:, own_cols(r, 0)] = jnp.concatenate([pbuf[7, 0] + ybuf[2], pad], axis=0).astype(BF16)

    diag = y_p + x_p - r

    def whole(q):
        return yt.at[:, chunk_cols(q)]

    def part_of(q, h):
        return yt.at[:, own_cols(q, h)]

    def gather_copy(k, ref, dev):
        return remote(ref, ref, gs_sem.at[k], gr_sem.at[k], rows_dev(dev))

    def relu_rows(q):
        cols = chunk_cols(q)
        keep = mask_ref[r, 2 * z + q // 4].astype(F32)
        rows = dot(yt[:, cols], w1p[...], ((0,), (0,)))
        zt[cols, :] = (jnp.maximum(rows, 0.0) * keep).astype(BF16)

    gather_copy(0, whole(r), x_p).start()
    gather_copy(1, whole(r), y_p).start()
    gather_copy(2, whole(r), core_p).start()
    relu_rows(r)
    gather_copy(2, whole(core_p), core_p).wait_recv()
    relu_rows(core_p)
    gather_copy(0, whole(x_p), x_p).wait_recv()
    gather_copy(3, part_of(x_p, 1), y_p).start()
    gather_copy(4, whole(x_p), core_p).start()
    gather_copy(1, whole(y_p), y_p).wait_recv()
    gather_copy(5, part_of(y_p, 0), x_p).start()
    gather_copy(6, whole(y_p), core_p).start()
    relu_rows(x_p)
    relu_rows(y_p)
    other = 1 - 2 * c
    gather_copy(4, whole(x_p + other), core_p).wait_recv()
    relu_rows(x_p + other)
    gather_copy(6, whole(y_p + other), core_p).wait_recv()
    relu_rows(y_p + other)
    gather_copy(3, part_of(diag, 1), y_p).wait_recv()
    gather_copy(5, part_of(diag, 0), x_p).wait_recv()
    gather_copy(7, whole(diag), core_p).start()
    relu_rows(diag)
    gather_copy(7, whole(diag + other), core_p).wait_recv()
    relu_rows(diag + other)

    low = z // 2
    step = 1 - 2 * low
    first_off = low * rows_half
    second_off = rows_half - first_off
    inner = rep_dev(lax.rem(z + step + 4, 4))
    outer = rep_dev(lax.rem(z - step + 4, 4))
    is_end = lax.rem(z, 3) == 0
    is_mid = lax.rem(z, 3) != 0

    def rows_at(off, n, size):
        return pl.ds(pl.multiple_of(off + n * size, 64), size)

    def first_rows(u):
        return rows_at(first_off, u, SUB)

    def second_rows(u):
        return rows_at(second_off, u, SUB)

    def slot(u):
        return rows_at(0, u, SUB)

    def first_end(u):
        return remote(y2.at[first_rows(u)], r_first.at[slot(u)], fs_sem.at[u], fr_sem.at[u], inner)

    def first_mid(u):
        return remote(y2.at[first_rows(u)], r_second.at[slot(u)], fs_sem.at[u], sr_sem.at[u], inner)

    def second_mid(u):
        return remote(y2.at[second_rows(u)], r_second.at[slot(u)], ss_sem.at[u], sr_sem.at[u], outer)

    def second_out(v):
        return ot.at[:, pl.ds(pl.multiple_of(second_off + v * OUT_COLS, 128), OUT_COLS)]

    def first_out(v):
        return ot.at[:, pl.ds(pl.multiple_of(first_off + v * OUT_COLS, 128), OUT_COLS)]

    def out_end(v):
        return remote(second_out(v), second_out(v), us_sem.at[v], ur_sem.at[v], inner)

    def out_mid(v):
        return remote(second_out(v), second_out(v), us_sem.at[v], vr_sem.at[v], inner)

    def out_last(v):
        return remote(first_out(v), first_out(v), vs_sem.at[v], vr_sem.at[v], outer)

    def event(it, carry):
        t = it - 4
        late = (t >= 2) & (t <= 11) & (lax.rem(t + 1, 3) == 0)

        @pl.when((it < 4) | late)
        def _():
            mi = jnp.where(it < 4, it, 4 + t // 3)
            is_second = (mi == 1) | (mi == 4) | (mi >= 6)
            m = jnp.where(mi == 1, 0, jnp.where(mi == 2, 1, jnp.where(mi == 3, 2, jnp.where(
                mi == 4, 1, jnp.where(mi == 5, 3, jnp.where(mi == 6, 2, jnp.where(mi == 7, 3, 0)))))))
            off = jnp.where(is_second, second_off, first_off)
            rows = rows_at(off, m, mm_rows)
            y2[rows, :] = dot(adj[rows, :], zt[...], ((1,), (0,)))

            @pl.when(is_end & jnp.logical_not(is_second))
            def _():
                def send(u, carry):
                    first_end(m * sub_mm + u).start()
                    return carry

                lax.fori_loop(0, sub_mm, send, 0)

        @pl.when(is_mid & (t >= 0) & (t < n_sub))
        def _():
            u = t
            first_end(u).wait_recv()
            y2[first_rows(u), :] = y2[first_rows(u), :] + r_first[slot(u), :]
            first_mid(u).start()

        @pl.when(is_mid & (t >= S_LAG) & (t < n_sub + S_LAG))
        def _():
            u = t - S_LAG
            first_mid(u).wait_recv()
            y2[second_rows(u), :] = y2[second_rows(u), :] + r_second[slot(u), :]
            second_mid(u).start()

        @pl.when(is_mid & (t >= OS_LAG) & (t < n_sub + OS_LAG) & (lax.rem(t - OS_LAG + 64, out_sub) == 0))
        def _():
            v = (t - OS_LAG) // out_sub
            out_end(v).wait_recv()
            out_mid(v).start()

        @pl.when(is_mid & (t >= OF_LAG) & (t < n_sub + OF_LAG) & (lax.rem(t - OF_LAG + 64, out_sub) == 0))
        def _():
            v = (t - OF_LAG) // out_sub
            out_mid(v).wait_recv()
            out_last(v).start()

        @pl.when(is_end & (t >= 12) & (t < n_sub + 12) & (lax.rem(t - 12 + 64, out_sub) == out_sub - 1))
        def _():
            v = (t - 12) // out_sub
            for i in range(out_sub):
                second_mid(v * out_sub + i).wait_recv()
            rows = rows_at(second_off, v, OUT_COLS)
            total = (y2[rows, :] + r_second[rows_at(0, v, OUT_COLS), :]).astype(BF16)
            second_out(v)[...] = dot(w2p[...], total, ((1,), (1,)))
            out_end(v).start()

        return carry

    lax.fori_loop(0, n_sub + OF_LAG + 4, event, 0)

    for k in range(4):
        core_copy(k).wait_send()
    x_copy(0, pbuf.at[4, 0]).wait_send()
    x_copy(1, pbuf.at[5, 0]).wait_send()
    x_copy(2, pbuf.at[5, 1]).wait_send()
    y_copy(0, pbuf.at[4, 1]).wait_send()
    y_copy(1, pbuf.at[6, 1]).wait_send()
    y_copy(2, pbuf.at[6, 0]).wait_send()
    for k, ref in ((0, whole(r)), (1, whole(r)), (2, whole(r)), (3, part_of(x_p, 1)), (4, whole(x_p)),
                   (5, part_of(y_p, 0)), (6, whole(y_p)), (7, whole(diag))):
        gather_copy(k, ref, core_p).wait_send()

    def drain_sub(u, carry):
        @pl.when(is_end)
        def _():
            first_end(u).wait_send()

        @pl.when(is_mid)
        def _():
            first_mid(u).wait_send()
            second_mid(u).wait_send()

        return carry

    lax.fori_loop(0, n_sub, drain_sub, 0)

    def drain_out(v, carry):
        @pl.when(is_end)
        def _():
            out_last(v).wait_recv()
            out_end(v).wait_send()

        @pl.when(is_mid)
        def _():
            out_mid(v).wait_send()
            out_last(v).wait_send()

        return carry

    lax.fori_loop(0, n_out, drain_out, 0)
    outt_ref[...] = ot[0:f2, :]


def solution(mesh):
    def local_fn(adj_local, block_mask, feat_blk, w_one, w_two):
        blk, width = adj_local.shape
        f0, f1 = w_one.shape
        f2 = w_two.shape[1]
        f0s = -(-f0 // 8) * 8
        f0p = -(-f0 // 16) * 16
        f2p = -(-f2 // 16) * 16
        chunk, rows_half = width // 8, blk // 2
        half = chunk // 2
        n_sub, n_out = rows_half // SUB, rows_half // OUT_COLS
        vmem = pl.BlockSpec(memory_space=pltpu.VMEM)
        dma = pltpu.SemaphoreType.DMA
        outt = pl.pallas_call(
            kernel,
            out_shape=jax.ShapeDtypeStruct((f2, blk), F32),
            in_specs=[pl.BlockSpec(memory_space=pltpu.SMEM), pl.BlockSpec(memory_space=pl.ANY), vmem, vmem, vmem],
            out_specs=vmem,
            scratch_shapes=[
                pltpu.VMEM((blk, width), BF16),
                pltpu.VMEM((f0p, blk), BF16),
                pltpu.VMEM((f0p, f1), BF16),
                pltpu.VMEM((f2p, f1), BF16),
                pltpu.VMEM((8, 2, f0s, half), F32),
                pltpu.VMEM((4, 2, f0s, half), F32),
                pltpu.VMEM((3, f0s, half), F32),
                pltpu.VMEM((3, f0s, half), F32),
                pltpu.VMEM((f0p, width), BF16),
                pltpu.VMEM((width, f1), BF16),
                pltpu.VMEM((blk, f1), F32),
                pltpu.VMEM((rows_half, f1), F32),
                pltpu.VMEM((rows_half, f1), F32),
                pltpu.VMEM((f2p, blk), F32),
                dma((8,)),
                dma((4,)), dma((4,)),
                dma((3,)), dma((3,)), dma((3,)), dma((3,)),
                dma((8,)), dma((8,)),
                dma((n_sub,)), dma((n_sub,)), dma((n_sub,)), dma((n_sub,)),
                dma((n_out,)), dma((n_out,)), dma((n_out,)), dma((n_out,)),
            ],
            compiler_params=pltpu.CompilerParams(collective_id=0, has_side_effects=True, vmem_limit_bytes=63 * 1024 * 1024),
        )(block_mask, adj_local, feat_blk.T, w_one, w_two.T)
        return outt.T

    return jax.shard_map(local_fn, mesh=mesh, in_specs=(P('rows', 'rep'), P(), P('rows', None), P(), P()), out_specs=P('rows', None), check_vma=False)
```

time: 320 us -> 113 us (0.35)
  blocking collectives: 164 us -> 0 us
  Pallas kernels: 0 us -> 111 us
  waiting for transfers between devices: 97.2 us -> 0 us
  matrix products: 39.5 us -> 0 us
  between operations: 13.5 us -> 0.01 us
    psum x2 -> x0, blocking collectives: 164 us -> none  [aggregate(): return lax.psum(part_sum, 'rep').astype(jnp.bfloat16)]
    pallas_call x0 -> x1, Pallas kernels: none -> 111 us  [local_fn(): pl.pallas_call(kernel, out_shape=jax.ShapeDtypeStruct((f2, blk), F32), in...]
    all_gather x2 -> x0, waiting for transfers between devices: 97.1 us -> none  [range_rows(): return lax.all_gather(recv_piece, 'rows', axis=0, tiled=True)]
    dot_general x4 -> x0, matrix products: 39.5 us -> none  [the longest x2 37.7 us: aggregate(): part_sum = jnp.dot(adj_local, masked, preferred_element_type=jnp.float32)]
  transfers between devices with their start and end apart: 4 -> 0, of which waited for: 2 -> 0; matrix products, arithmetic and copies ran while one was open for 0% -> 0% of each run, Pallas kernels for 0% -> 0%
where the time goes in v1:
time: 113 us
  Pallas kernels  111 us (98%)
  local copies, waits for them, and re-layouts  1.92 us (2%)
    pallas_call x1, Pallas kernels, local_fn(): pl.pallas_call(kernel, out_shape=jax.ShapeDtypeStruct((f2, blk), F32), in...  111 us

profile of v1, /device:TPU:0, one launch (start us, length us, event | category | flops | bytes accessed | tf_op | source)
XLA Modules:
  0.0 112.6 jit_solution(2472203298095145026)
XLA Ops:
  0.0 110.7 %shard_map.55 = f32[47,3072]{1,0:T(8,128)} custom-call(s32[8,8]{1,0:T(8,128)} %mask_ref.1, bf16[3072,6144]{1,0:T(8,128)(2,1)} %adj_hbm.1, bf16[100,3072]{1,0:T(8,128)(2,1)} %bitcast.4, bf16[100,256]{1,0:T(8,128)(2,1)} %w1_ref.1, bf16[47,256]{1,0:T(8,128)(2,1)} %bitcast.5), custom_call_target="tpu_custom_call" | custom-call | tf_op jit(solution)/shard_map/pallas_call | solution.py:368
  110.7 1.9 %copy.7 = f32[3072,47]{0,1:T(8,128)} copy(f32[3072,47]{0,1:T(8,128)} %bitcast.3) | data formatting | bytes 1155072
